TPU v7x, 32 devices: a whole 2x2x4 slice. The times are simulated.
32 devices in a mesh: wide: 8 (over z, x), narrow: 4 (over y, core).
Axes of the slice: x: 2, y: 2, z: 4, core: 2. Of those that a mesh axis runs over, the one named last changes fastest.
Arguments:
- positions: float32 [3, 4096], P(None, ('wide', 'narrow')), may hold values from -1 to 69, as said below
- noise: float32 [3, 16, 4096], P(None, None, ('wide', 'narrow')), may hold values from -6 to 6
Outputs:
- displacement: float32 [3, 16, 4096], P(None, None, ('wide', 'narrow'))
Inputs may be any that keep to these rules, and one draw needn't show every extreme that they name: `positions`: any two particles lie at least 1.2 apart.
All inputs are finite; a program needn't handle non-finite values.
Results may differ from a plain program's by a relative error of at most 0.0003.
Values sent between devices are 32-bit elements; how exact they have to be, the bound alone decides.
A program may use at most 64 MiB of HBM per device.

v0:
```python
import math
import jax
import jax.numpy as jnp
from jax import lax
from jax.sharding import PartitionSpec as P

ITERS = 3
ROOT_STEPS = 30
highest = lax.Precision.HIGHEST


def tile_factors(dist_sq, itself):
    safe_sq = jnp.where(itself, 4.0, dist_sq)
    radial = jnp.sqrt(safe_sq)
    inverse = 1.0 / radial
    far_scalar = 0.75 * inverse + 0.5 * inverse * inverse * inverse
    far_outer = (0.75 * inverse - 1.5 * inverse * inverse * inverse) * inverse * inverse
    near_scalar = 1.0 - 0.28125 * radial
    near_outer = 0.09375 * inverse
    nearby = radial < 2.0
    scalar = jnp.where(itself, 1.0, jnp.where(nearby, near_scalar, far_scalar))
    outer_part = jnp.where(itself, 0.0, jnp.where(nearby, near_outer, far_outer))
    return (scalar, outer_part)


def contract(left, kernel):
    return lax.dot_general(
        left,
        kernel,
        (((1,), (1,)), ((), ())),
        precision=highest,
        preferred_element_type=jnp.float32,
    )


def tile_product(row_pos, row_ids, col_pos, col_ids, vectors):
    width = vectors.shape[1]
    delta = row_pos[:, :, None] - col_pos[:, None, :]
    dist_sq = delta[0] * delta[0] + delta[1] * delta[1] + delta[2] * delta[2]
    itself = row_ids[:, None] == col_ids[None, :]
    scalar, outer_part = tile_factors(dist_sq, itself)
    result = []
    for component in range(3):
        diag_kernel = scalar + outer_part * delta[component] * delta[component]
        result.append(contract(vectors[component], diag_kernel))
    for first, second in ((0, 1), (0, 2), (1, 2)):
        cross = outer_part * delta[first] * delta[second]
        both = contract(jnp.concatenate([vectors[second], vectors[first]], axis=0), cross)
        result[first] = result[first] + both[:width]
        result[second] = result[second] + both[width:]
    return jnp.stack(result)


def blocked_product(row_pos, row_ids, col_pos, col_ids, vectors):
    rows = row_pos.shape[1]
    block = math.gcd(rows, 512)

    def row_block(index):
        begin = index * block
        pos_block = lax.dynamic_slice_in_dim(row_pos, begin, block, 1)
        id_block = lax.dynamic_slice_in_dim(row_ids, begin, block, 0)
        return tile_product(pos_block, id_block, col_pos, col_ids, vectors)

    pieces = lax.map(row_block, jnp.arange(rows // block, dtype=jnp.int32))
    return jnp.moveaxis(pieces, 0, 2).reshape(3, vectors.shape[1], rows)


def gram_of(left, right):
    return jnp.einsum("asp,atp->st", left, right, precision=highest)


def stacked_gram(stacked, right):
    return jnp.einsum("kasp,atp->kst", stacked, right, precision=highest)


def stacked_remove(stacked, weights):
    return jnp.einsum("kasp,kst->atp", stacked, weights, precision=highest)


def block_remove(member, weights):
    return jnp.einsum("asp,st->atp", member, weights, precision=highest)


def rotate(block, matrix):
    return jnp.einsum("atp,ts->asp", block, matrix, precision=highest)


def cholesky_pair(gram):
    order = gram.shape[0]
    places = jnp.arange(order, dtype=jnp.int32)
    lower = jnp.zeros((order, order), jnp.float32)
    for column in range(order):
        needed = gram[:, column] - jnp.dot(
            lower, lower[column, :], precision=highest, preferred_element_type=jnp.float32
        )
        pivot = jnp.sqrt(needed[column])
        entries = jnp.where(places >= column, needed / pivot, 0.0)
        marker = (places == column).astype(jnp.float32)
        lower = lower + entries[:, None] * marker[None, :]
    solved = jnp.zeros((order, order), jnp.float32)
    for row in range(order):
        marker = (places == row).astype(jnp.float32)
        fresh = (
            marker
            - jnp.dot(lower[row, :], solved, precision=highest, preferred_element_type=jnp.float32)
        ) / lower[row, row]
        solved = solved + marker[:, None] * fresh[None, :]
    return (lower.T, solved.T)


def tridiagonal(diagonal_blocks, lower_blocks):
    width = diagonal_blocks[0].shape[0]
    order = len(diagonal_blocks) * width
    matrix = jnp.zeros((order, order), jnp.float32)
    for index, block in enumerate(diagonal_blocks):
        offset = index * width
        matrix = matrix.at[offset : offset + width, offset : offset + width].set(block)
    for index, block in enumerate(lower_blocks):
        offset = index * width
        matrix = matrix.at[offset + width : offset + 2 * width, offset : offset + width].set(block)
        matrix = matrix.at[offset : offset + width, offset + width : offset + 2 * width].set(
            block.T
        )
    return matrix


def matrix_root(matrix):
    identity = jnp.eye(matrix.shape[0], dtype=jnp.float32)
    scale = jnp.sqrt(jnp.sum(matrix * matrix))

    def newton(turn, carry):
        current, other = carry
        factor = 1.5 * identity - 0.5 * jnp.dot(
            other, current, precision=highest, preferred_element_type=jnp.float32
        )
        return (
            jnp.dot(current, factor, precision=highest, preferred_element_type=jnp.float32),
            jnp.dot(factor, other, precision=highest, preferred_element_type=jnp.float32),
        )

    current, other = lax.fori_loop(0, ROOT_STEPS, newton, (matrix / scale, identity))
    return current * jnp.sqrt(scale)


def first_pass(basis, image):
    work = image
    single = None
    for member in basis:
        single = lax.psum(gram_of(member, work), ("wide", "narrow"))
        work = work - block_remove(member, single)
    return (single, work)


def second_pass(basis, work):
    stacked = jnp.stack(basis)
    again, raw_gram = lax.psum(
        (stacked_gram(stacked, work), gram_of(work, work)), ("wide", "narrow")
    )
    work = work - stacked_remove(stacked, again)
    gram = raw_gram - jnp.einsum("kst,ksu->tu", again, again, precision=highest)
    return (work, gram)


def per_device(positions, noise):
    width = noise.shape[1]
    local = noise.shape[2]
    narrow_count = lax.axis_size("narrow")
    row_pos = lax.all_gather(positions, "narrow", axis=1, tiled=True)
    col_pos = lax.all_gather(positions, "wide", axis=1, tiled=True)
    row_ids = lax.axis_index("wide") * (narrow_count * local) + jnp.arange(
        narrow_count * local, dtype=jnp.int32
    )
    places = jnp.arange(col_pos.shape[1], dtype=jnp.int32)
    col_ids = (
        places // local * (narrow_count * local) + lax.axis_index("narrow") * local + places % local
    )
    noise_gram = lax.psum(gram_of(noise, noise), ("wide", "narrow"))
    start_upper, start_inverse = cholesky_pair(noise_gram)
    basis = [rotate(noise, start_inverse)]
    diagonal_blocks = []
    lower_blocks = []
    for index in range(ITERS):
        empty = jnp.zeros((3, width, row_pos.shape[1]), jnp.float32)
        partial_rows = empty + blocked_product(
            row_pos,
            row_ids,
            col_pos,
            col_ids,
            lax.all_gather(basis[index], "wide", axis=2, tiled=True),
        )
        product = lax.psum_scatter(partial_rows, "narrow", scatter_dimension=2, tiled=True)
        if index + 1 == ITERS:
            current_block = lax.psum(gram_of(basis[index], product), ("wide", "narrow"))
            diagonal_blocks.append(0.5 * (current_block + current_block.T))
        else:
            current_block, work = first_pass(basis, product)
            diagonal_blocks.append(0.5 * (current_block + current_block.T))
            work, gram = second_pass(basis, work)
            upper, inverse = cholesky_pair(gram)
            lower_blocks.append(upper)
            basis.append(rotate(work, inverse))
    root = matrix_root(tridiagonal(diagonal_blocks, lower_blocks))
    mixing = jnp.dot(
        root[:, :width], start_upper, precision=highest, preferred_element_type=jnp.float32
    ).reshape(ITERS, width, width)
    return jnp.einsum("katp,kts->asp", jnp.stack(basis), mixing, precision=highest)


def solution(mesh):
    return jax.shard_map(
        per_device,
        mesh=mesh,
        in_specs=(P(None, ("wide", "narrow")), P(None, None, ("wide", "narrow"))),
        out_specs=P(None, None, ("wide", "narrow")),
        check_vma=False,
    )
```

profile of v0, /device:TPU:0, one launch (start us, length us, event | category | flops | bytes accessed | tf_op | source)
XLA Modules:
  0.0 678.2 jit_solution(14943982212568380633)
XLA Ops:
  6.5 28.2 %all_gather.17 = f32[3,1024]{1,0:T(4,128)S(1)} all-gather(f32[3,128]{1,0:T(4,128)} %param.18), channel_id=1, replica_groups=mesh['wide'=8,'narrow'=4] {'wide'}, dimensions={1}, use_global_device_ids=true | all-gather | bytes 13824 | tf_op jit(solution)/shard_map/all_gather | solution.py:169
  34.7 5.3 all_gather.16
  40.5 4.1 fusion.9
  44.6 3.1 bitcast_multiply_fusion.4
  47.8 2.9 bitcast_multiply_fusion.1
  50.9 38.9 %psum.63 = f32[16,16]{1,0:T(8,128)S(1)} all-reduce(f32[16,16]{1,0:T(8,128)S(1)} %convolution_bitcast_fusion.16), channel_id=1, replica_groups=mesh['wide'=8,'narrow'=4] {'wide','narrow'}, use_global_device_ids=true, to_apply=%region_0.1 | all-reduce | flops 256 | bytes 2048 | tf_op jit(solution)/shard_map/psum | solution.py:177
  128.0 30.8 %all_gather.15 = f32[3,16,1024]{2,1,0:T(8,128)S(1)} all-gather(f32[3,16,128]{2,1,0:T(8,128)S(1)} %bitcast.1264), channel_id=1, replica_groups=mesh['wide'=8,'narrow'=4] {'wide'}, dimensions={2}, use_global_device_ids=true | all-gather | bytes 221184 | tf_op jit(solution)/shard_map/all_gather | solution.py:189
  158.8 3.7 fusion.190
  162.6 2.0 fusion.192
  164.6 2.0 fusion.191
  166.6 3.2 fusion.13
  177.5 17.6 %reduce-scatter.4.cloned.1.call-done = f32[3,16,128]{2,1,0:T(8,128)} async-done(((f32[3,16,512]{2,1,0:T(8,128)}), f32[3,16,128]{2,1,0:T(8,128)}) %reduce-scatter.4.cloned.1.call-update) | async-done | bytes 24592 | tf_op jit(solution)/shard_map/reduce_scatter | solution.py:191
  196.0 39.4 %psum.64 = f32[16,16]{1,0:T(8,128)S(1)} all-reduce(f32[16,16]{1,0:T(8,128)S(1)} %convolution_bitcast_fusion.15), channel_id=1, replica_groups=mesh['wide'=8,'narrow'=4] {'wide','narrow'}, use_global_device_ids=true, to_apply=%region_2.3 | all-reduce | flops 256 | bytes 2048 | tf_op jit(solution)/shard_map/psum | solution.py:149
  236.6 41.5 %all-reduce.2 = (f32[16,16]{1,0:T(8,128)S(1)}, f32[16,16]{1,0:T(8,128)S(1)}) all-reduce(f32[16,16]{1,0:T(8,128)S(1)} %convolution_bitcast_fusion.13, f32[16,16]{1,0:T(8,128)S(1)} %convolution_bitcast_fusion.14), channel_id=1, replica_groups=mesh['wide'=8,'narrow'=4] {'wide','narrow'}, use_global_device_ids=true, to_apply=%region_4.5 | all-reduce | flops 512 | bytes 4096 | tf_op jit(solution)/shard_map/psum | solution.py:156
  316.6 30.6 %all_gather.18 = f32[3,16,1024]{2,1,0:T(8,128)S(1)} all-gather(f32[3,16,128]{2,1,0:T(8,128)S(1)} %bitcast.1268), channel_id=1, replica_groups=mesh['wide'=8,'narrow'=4] {'wide'}, dimensions={2}, use_global_device_ids=true | all-gather | bytes 221184 | tf_op jit(solution)/shard_map/all_gather | solution.py:189
  347.3 2.0 fusion.187
  349.3 2.0 fusion.189
  351.4 2.0 fusion.188
  359.9 19.5 %reduce-scatter.6.cloned.1.call-done = f32[3,16,128]{2,1,0:T(8,128)} async-done(((f32[3,16,512]{2,1,0:T(8,128)}), f32[3,16,128]{2,1,0:T(8,128)}) %reduce-scatter.6.cloned.1.call-update) | async-done | bytes 24592 | tf_op jit(solution)/shard_map/reduce_scatter | solution.py:191
  380.3 39.4 %psum.67 = f32[16,16]{0,1:T(8,128)S(1)} all-reduce(f32[16,16]{0,1:T(8,128)S(1)} %convolution_bitcast_fusion.12), channel_id=1, replica_groups=mesh['wide'=8,'narrow'=4] {'wide','narrow'}, use_global_device_ids=true, to_apply=%region_6.7 | all-reduce | flops 256 | bytes 2048 | tf_op jit(solution)/shard_map/psum | solution.py:149
  420.7 41.1 %psum.68 = f32[16,16]{0,1:T(8,128)S(1)} all-reduce(f32[16,16]{0,1:T(8,128)S(1)} %convolution_bitcast_fusion.11), channel_id=1, replica_groups=mesh['wide'=8,'narrow'=4] {'wide','narrow'}, use_global_device_ids=true, to_apply=%region_7.8 | all-reduce | flops 256 | bytes 2048 | tf_op jit(solution)/shard_map/psum | solution.py:149
  462.3 39.5 %all-reduce.1 = (f32[2,16,16]{2,1,0:T(8,128)S(1)}, f32[16,16]{1,0:T(8,128)S(1)}) all-reduce(f32[2,16,16]{2,1,0:T(8,128)S(1)} %convolution_bitcast_fusion.7, f32[16,16]{1,0:T(8,128)S(1)} %convolution_bitcast_fusion.10), channel_id=1, replica_groups=mesh['wide'=8,'narrow'=4] {'wide','narrow'}, use_global_device_ids=true, to_apply=%region_9.10 | all-reduce | flops 768 | bytes 6144 | tf_op jit(solution)/shard_map/psum | solution.py:156
  540.3 30.8 %all_gather.19 = f32[3,16,1024]{2,1,0:T(8,128)S(1)} all-gather(f32[3,16,128]{2,1,0:T(8,128)S(1)} %bitcast.1272), channel_id=1, replica_groups=mesh['wide'=8,'narrow'=4] {'wide'}, dimensions={2}, use_global_device_ids=true | all-gather | bytes 221184 | tf_op jit(solution)/shard_map/all_gather | solution.py:189
  571.1 2.0 fusion.184
  573.1 2.0 fusion.186
  575.2 2.0 fusion.185
  580.9 1.9 fusion.32
  584.3 19.2 %reduce-scatter.8.cloned.1.call-done = f32[3,16,128]{2,1,0:T(8,128)} async-done(((f32[3,16,512]{2,1,0:T(8,128)}), f32[3,16,128]{2,1,0:T(8,128)}) %reduce-scatter.8.cloned.1.call-update) | async-done | bytes 24592 | tf_op jit(solution)/shard_map/reduce_scatter | solution.py:191
  604.4 39.6 %psum.71 = f32[16,16]{0,1:T(8,128)S(1)} all-reduce(f32[16,16]{0,1:T(8,128)S(1)} %convolution_bitcast_fusion.8), channel_id=1, replica_groups=mesh['wide'=8,'narrow'=4] {'wide','narrow'}, use_global_device_ids=true, to_apply=%region_11.12 | all-reduce | flops 256 | bytes 2048 | tf_op jit(solution)/shard_map/psum | solution.py:193
  645.4 1.9 dynamic-slice_select_fusion
  647.3 2.0 scatter.30
  652.4 17.9 %while.15 = (s32[]{:T(128)}, f32[48,48]{0,1:T(8,128)S(1)}, f32[48,48]{1,0:T(8,128)S(1)}, s32[]{:T(128)}) while((s32[]{:T(128)}, f32[48,48]{0,1:T(8,128)S(1)}, f32[48,48]{1,0:T(8,128)S(1)}, s32[]{:T(128)}) %tuple.168), condition=%wide.region_15.16_spmd.clone, body=%wide.region_14.15_spmd.clone.sunk | while | flops 3990530 | bytes 119861 | solution.py:141
  (507 shorter events, 129.4 us)
Async XLA Ops:
  6.5 44.2 %copy-start = (f32[3,16,128]{2,1,0:T(8,128)S(1)}, f32[3,16,128]{2,1,0:T(8,128)}, u32[]{:S(2)}) copy-start(f32[3,16,128]{2,1,0:T(8,128)} %param.19) | copy-start | bytes 73732
  6.5 188.5 %reduce-scatter.4.cloned.1.call-start = ((), (), s32[]{:S(2)}) async-start(), calls=%async_computation.3 | async-start | bytes 122880 | tf_op jit(solution)/shard_map/reduce_scatter | solution.py:191
  40.5 7.3 %copy-start.1 = (f32[3,512,1024]{2,1,0:T(8,128)}, f32[3,512,1024]{2,1,0:T(8,128)S(1)}, u32[]{:S(2)}) copy-start(f32[3,512,1024]{2,1,0:T(8,128)S(1)} %broadcast_subtract_fusion) | copy-start | bytes 18874372
  110.4 52.2 %copy-start.6 = (f32[512,1024]{1,0:T(8,128)S(1)}, f32[512,1024]{1,0:T(8,128)}, u32[]{:S(2)}) copy-start(f32[512,1024]{1,0:T(8,128)} %get-tuple-element.254) | copy-start | bytes 6291460
  122.6 42.0 %copy-start.3 = (f32[512,1024]{1,0:T(8,128)S(1)}, f32[512,1024]{1,0:T(8,128)}, u32[]{:S(2)}) copy-start(f32[512,1024]{1,0:T(8,128)} %get-tuple-element.250) | copy-start | bytes 6291460
  158.8 7.8 %copy-start.2 = (f32[3,512,1024]{2,1,0:T(8,128)S(1)}, f32[3,512,1024]{2,1,0:T(8,128)}, u32[]{:S(2)}) copy-start(f32[3,512,1024]{2,1,0:T(8,128)} %copy-done.1) | copy-start | bytes 18874372
  169.9 3.7 copy-start.11
  169.9 3.7 copy-start.14
  176.2 203.2 %reduce-scatter.6.cloned.1.call-start = ((), (), s32[]{:S(2)}) async-start(), calls=%async_computation.4 | async-start | bytes 122880 | tf_op jit(solution)/shard_map/reduce_scatter | solution.py:191
  280.8 66.5 %copy-start.9 = (f32[512,1024]{1,0:T(8,128)S(1)}, f32[512,1024]{1,0:T(8,128)}, u32[]{:S(2)}) copy-start(f32[512,1024]{1,0:T(8,128)} %get-tuple-element.255) | copy-start | bytes 6291460
  309.6 39.7 %copy-start.7 = (f32[512,1024]{1,0:T(8,128)S(1)}, f32[512,1024]{1,0:T(8,128)}, u32[]{:S(2)}) copy-start(f32[512,1024]{1,0:T(8,128)} %get-tuple-element.254) | copy-start | bytes 6291460
  347.3 4.1 copy-start.4
  349.3 4.1 copy-start.15
  351.4 3.9 copy-start.12
  359.7 243.9 %reduce-scatter.8.cloned.1.call-start = ((), (), s32[]{:S(2)}) async-start(), calls=%async_computation.5 | async-start | bytes 122880 | tf_op jit(solution)/shard_map/reduce_scatter | solution.py:191
  504.4 66.6 %copy-start.10 = (f32[512,1024]{1,0:T(8,128)S(1)}, f32[512,1024]{1,0:T(8,128)}, u32[]{:S(2)}) copy-start(f32[512,1024]{1,0:T(8,128)} %get-tuple-element.255) | copy-start | bytes 6291460
  533.2 39.9 %copy-start.8 = (f32[512,1024]{1,0:T(8,128)S(1)}, f32[512,1024]{1,0:T(8,128)}, u32[]{:S(2)}) copy-start(f32[512,1024]{1,0:T(8,128)} %get-tuple-element.254) | copy-start | bytes 6291460
  571.1 4.1 copy-start.5
  573.1 4.1 copy-start.16
  575.1 3.9 copy-start.13
Sparse Core Ops, SparseCore 0:
  176.3 18.7 reduce-scatter.3
  359.8 19.4 reduce-scatter.5
  583.5 20.0 reduce-scatter.7
where the time goes:
time: 686 us; the launch traced here: 678 us
  blocking collectives  405 us (59%)
  matrix products  107 us (16%)
  waiting for transfers between devices  56.3 us (8%)
  between operations  46.8 us (7%)
  local copies, waits for them, and re-layouts  37.3 us (5%)
  other arithmetic  24.4 us (4%)
    psum x3, blocking collectives, first_pass(): single = lax.psum(gram_of(member, work), ('wide', 'narrow'))  120 us
    all_gather x3, blocking collectives, per_device(): lax.all_gather(basis[index], 'wide', axis=2, tiled=True)  92.2 us
    psum x2, blocking collectives, second_pass(): lax.psum((stacked_gram(stacked, work), gram_of(work, work)), ('wide', 'na...  81 us
    reduce_scatter x3, waiting for transfers between devices, per_device(): lax.psum_scatter(partial_rows, 'narrow', scatter_dimension=2, tiled=True)  56.3 us
    psum x1, blocking collectives, per_device(): current_block = lax.psum(gram_of(basis[index], product), ('wide', 'narrow'))  39.6 us
    dot_general x48, matrix products, cholesky_pair(): jnp.dot(lower[row, :], solved, precision=highest, preferred_element_type=...  39.5 us
    psum x1, blocking collectives, per_device(): noise_gram = lax.psum(gram_of(noise, noise), ('wide', 'narrow'))  38.9 us
    dot_general x18, matrix products, contract(): lax.dot_general(left, kernel, (((1,), (1,)), ((), ())), precision=highest...  36.4 us
  transfers between devices with their start and end apart: 3, of which 3 were waited for; matrix products, arithmetic and copies ran while one was open for 0% of the time, Pallas kernels for 0%

commit v1 on v0

--- a/solution.py
+++ b/solution.py
@@ -146,7 +146,7 @@
     work = image
     single = None
     for member in basis:
-        single = lax.psum(gram_of(member, work), ("wide", "narrow"))
+        single = jnp.sum(lax.all_gather(gram_of(member, work), ("wide", "narrow")), axis=0)
         work = work - block_remove(member, single)
     return (single, work)
 

time: 686 us -> 681 us (level)
    all_gather x0 -> x3, blocking collectives: none -> 120 us  [first_pass(): lax.all_gather(gram_of(member, work), ('wide', 'narrow'))]
    psum x3 -> x0, blocking collectives: 120 us -> none  [first_pass(): single = lax.psum(gram_of(member, work), ('wide', 'narrow'))]
where the time goes in v1:
time: 681 us; the launch traced here: 673 us
  blocking collectives  399 us (59%)
  matrix products  107 us (16%)
  waiting for transfers between devices  56.7 us (8%)
  between operations  47 us (7%)
  local copies, waits for them, and re-layouts  37.3 us (5%)
  other arithmetic  24.5 us (4%)
    all_gather x3, blocking collectives, first_pass(): lax.all_gather(gram_of(member, work), ('wide', 'narrow'))  120 us
    all_gather x3, blocking collectives, per_device(): lax.all_gather(basis[index], 'wide', axis=2, tiled=True)  92.5 us
    psum x2, blocking collectives, second_pass(): lax.psum((stacked_gram(stacked, work), gram_of(work, work)), ('wide', 'na...  74.6 us
    reduce_scatter x3, waiting for transfers between devices, per_device(): lax.psum_scatter(partial_rows, 'narrow', scatter_dimension=2, tiled=True)  56.6 us
    psum x1, blocking collectives, per_device(): current_block = lax.psum(gram_of(basis[index], product), ('wide', 'narrow'))  39.6 us
    dot_general x48, matrix products, cholesky_pair(): jnp.dot(lower[row, :], solved, precision=highest, preferred_element_type=...  39.5 us
    psum x1, blocking collectives, per_device(): noise_gram = lax.psum(gram_of(noise, noise), ('wide', 'narrow'))  38.9 us
    dot_general x18, matrix products, contract(): lax.dot_general(left, kernel, (((1,), (1,)), ((), ())), precision=highest...  36.4 us
  transfers between devices with their start and end apart: 3, of which 3 were waited for; matrix products, arithmetic and copies ran while one was open for 0% of the time, Pallas kernels for 0%

profile of v1, /device:TPU:0, one launch (start us, length us, event | category | flops | bytes accessed | tf_op | source)
XLA Modules:
  0.0 673.0 jit_solution(2929327929122243327)
XLA Ops:
  6.5 28.2 %all_gather.35 = f32[3,1024]{1,0:T(4,128)S(1)} all-gather(f32[3,128]{1,0:T(4,128)} %param.18), channel_id=1, replica_groups=mesh['wide'=8,'narrow'=4] {'wide'}, dimensions={1}, use_global_device_ids=true | all-gather | bytes 13824 | tf_op jit(solution)/shard_map/all_gather | solution.py:169
  34.7 5.3 all_gather.34
  40.5 4.1 fusion.9
  44.6 3.1 bitcast_multiply_fusion.4
  47.8 2.9 bitcast_multiply_fusion.1
  50.9 38.9 %psum.42 = f32[16,16]{1,0:T(8,128)S(1)} all-reduce(f32[16,16]{1,0:T(8,128)S(1)} %convolution_bitcast_fusion.16), channel_id=1, replica_groups=mesh['wide'=8,'narrow'=4] {'wide','narrow'}, use_global_device_ids=true, to_apply=%region_0.1 | all-reduce | flops 256 | bytes 2048 | tf_op jit(solution)/shard_map/psum | solution.py:177
  128.0 31.2 %all_gather.33 = f32[3,16,1024]{2,1,0:T(8,128)S(1)} all-gather(f32[3,16,128]{2,1,0:T(8,128)S(1)} %bitcast.1267), channel_id=1, replica_groups=mesh['wide'=8,'narrow'=4] {'wide'}, dimensions={2}, use_global_device_ids=true | all-gather | bytes 221184 | tf_op jit(solution)/shard_map/all_gather | solution.py:189
  159.2 3.7 fusion.190
  162.9 2.0 fusion.192
  165.0 2.0 fusion.191
  167.0 3.2 fusion.13
  172.1 1.9 fusion.22
  177.8 17.6 %reduce-scatter.4.cloned.1.call-done = f32[3,16,128]{2,1,0:T(8,128)} async-done(((f32[3,16,512]{2,1,0:T(8,128)}), f32[3,16,128]{2,1,0:T(8,128)}) %reduce-scatter.4.cloned.1.call-update) | async-done | bytes 24592 | tf_op jit(solution)/shard_map/reduce_scatter | solution.py:191
  196.3 41.2 %all-gather = f32[512,16]{1,0:T(8,128)S(1)} all-gather(f32[16,16]{1,0:T(8,128)S(1)} %convolution_bitcast_fusion.15), channel_id=2, replica_groups=mesh['wide'=8,'narrow'=4] {'wide','narrow'}, dimensions={0}, use_global_device_ids=true | all-gather | bytes 33792 | tf_op jit(solution)/shard_map/all_gather | solution.py:149
  238.8 37.2 %all-reduce.2 = (f32[16,16]{1,0:T(8,128)S(1)}, f32[16,16]{1,0:T(8,128)S(1)}) all-reduce(f32[16,16]{1,0:T(8,128)S(1)} %convolution_bitcast_fusion.13, f32[16,16]{1,0:T(8,128)S(1)} %convolution_bitcast_fusion.14), channel_id=1, replica_groups=mesh['wide'=8,'narrow'=4] {'wide','narrow'}, use_global_device_ids=true, to_apply=%region_4.5 | all-reduce | flops 512 | bytes 4096 | tf_op jit(solution)/shard_map/psum | solution.py:156
  314.5 30.7 %all_gather.38 = f32[3,16,1024]{2,1,0:T(8,128)S(1)} all-gather(f32[3,16,128]{2,1,0:T(8,128)S(1)} %bitcast.1274), channel_id=1, replica_groups=mesh['wide'=8,'narrow'=4] {'wide'}, dimensions={2}, use_global_device_ids=true | all-gather | bytes 221184 | tf_op jit(solution)/shard_map/all_gather | solution.py:189
  345.3 2.0 fusion.187
  347.4 2.0 fusion.189
  349.4 2.0 fusion.188
  357.9 19.3 %reduce-scatter.6.cloned.1.call-done = f32[3,16,128]{2,1,0:T(8,128)} async-done(((f32[3,16,512]{2,1,0:T(8,128)}), f32[3,16,128]{2,1,0:T(8,128)}) %reduce-scatter.6.cloned.1.call-update) | async-done | bytes 24592 | tf_op jit(solution)/shard_map/reduce_scatter | solution.py:191
  378.1 41.3 %all-gather.1 = f32[512,16]{1,0:T(8,128)S(1)} all-gather(f32[16,16]{1,0:T(8,128)S(1)} %convolution_bitcast_fusion.12), channel_id=3, replica_groups=mesh['wide'=8,'narrow'=4] {'wide','narrow'}, dimensions={0}, use_global_device_ids=true | all-gather | bytes 33792 | tf_op jit(solution)/shard_map/all_gather | solution.py:149
  420.6 37.4 %all-gather.2 = f32[512,16]{1,0:T(8,128)S(1)} all-gather(f32[16,16]{1,0:T(8,128)S(1)} %convolution_bitcast_fusion.11), channel_id=4, replica_groups=mesh['wide'=8,'narrow'=4] {'wide','narrow'}, dimensions={0}, use_global_device_ids=true | all-gather | bytes 33792 | tf_op jit(solution)/shard_map/all_gather | solution.py:149
  458.6 37.4 %all-reduce.1 = (f32[2,16,16]{2,1,0:T(8,128)S(1)}, f32[16,16]{1,0:T(8,128)S(1)}) all-reduce(f32[2,16,16]{2,1,0:T(8,128)S(1)} %convolution_bitcast_fusion.7, f32[16,16]{1,0:T(8,128)S(1)} %convolution_bitcast_fusion.10), channel_id=1, replica_groups=mesh['wide'=8,'narrow'=4] {'wide','narrow'}, use_global_device_ids=true, to_apply=%region_9.10 | all-reduce | flops 768 | bytes 6144 | tf_op jit(solution)/shard_map/psum | solution.py:156
  534.5 30.6 %all_gather.43 = f32[3,16,1024]{2,1,0:T(8,128)S(1)} all-gather(f32[3,16,128]{2,1,0:T(8,128)S(1)} %bitcast.1278), channel_id=1, replica_groups=mesh['wide'=8,'narrow'=4] {'wide'}, dimensions={2}, use_global_device_ids=true | all-gather | bytes 221184 | tf_op jit(solution)/shard_map/all_gather | solution.py:189
  565.1 2.0 fusion.184
  567.2 2.0 fusion.186
  569.2 2.0 fusion.185
  578.4 19.7 %reduce-scatter.8.cloned.1.call-done = f32[3,16,128]{2,1,0:T(8,128)} async-done(((f32[3,16,512]{2,1,0:T(8,128)}), f32[3,16,128]{2,1,0:T(8,128)}) %reduce-scatter.8.cloned.1.call-update) | async-done | bytes 24592 | tf_op jit(solution)/shard_map/reduce_scatter | solution.py:191
  599.0 39.6 %psum.47 = f32[16,16]{1,0:T(8,128)S(1)} all-reduce(f32[16,16]{1,0:T(8,128)S(1)} %convolution_bitcast_fusion.8), channel_id=1, replica_groups=mesh['wide'=8,'narrow'=4] {'wide','narrow'}, use_global_device_ids=true, to_apply=%region_11.12 | all-reduce | flops 256 | bytes 2048 | tf_op jit(solution)/shard_map/psum | solution.py:193
  639.9 1.9 dynamic-slice_select_fusion
  641.9 2.0 scatter.30
  646.9 17.9 %while.15 = (s32[]{:T(128)}, f32[48,48]{0,1:T(8,128)S(1)}, f32[48,48]{1,0:T(8,128)S(1)}, s32[]{:T(128)}) while((s32[]{:T(128)}, f32[48,48]{0,1:T(8,128)S(1)}, f32[48,48]{1,0:T(8,128)S(1)}, s32[]{:T(128)}) %tuple.169), condition=%wide.region_15.16_spmd.clone, body=%wide.region_14.15_spmd.clone.sunk | while | flops 3990530 | bytes 119861 | solution.py:141
  (510 shorter events, 129.6 us)
Async XLA Ops:
  6.5 44.2 %copy-start = (f32[3,16,128]{2,1,0:T(8,128)S(1)}, f32[3,16,128]{2,1,0:T(8,128)}, u32[]{:S(2)}) copy-start(f32[3,16,128]{2,1,0:T(8,128)} %param.19) | copy-start | bytes 73732
  6.5 188.9 %reduce-scatter.4.cloned.1.call-start = ((), (), s32[]{:S(2)}) async-start(), calls=%async_computation.3 | async-start | bytes 122880 | tf_op jit(solution)/shard_map/reduce_scatter | solution.py:191
  40.5 7.3 %copy-start.1 = (f32[3,512,1024]{2,1,0:T(8,128)}, f32[3,512,1024]{2,1,0:T(8,128)S(1)}, u32[]{:S(2)}) copy-start(f32[3,512,1024]{2,1,0:T(8,128)S(1)} %broadcast_subtract_fusion) | copy-start | bytes 18874372
  110.4 52.5 %copy-start.6 = (f32[512,1024]{1,0:T(8,128)S(1)}, f32[512,1024]{1,0:T(8,128)}, u32[]{:S(2)}) copy-start(f32[512,1024]{1,0:T(8,128)} %get-tuple-element.257) | copy-start | bytes 6291460
  122.6 42.4 %copy-start.3 = (f32[512,1024]{1,0:T(8,128)S(1)}, f32[512,1024]{1,0:T(8,128)}, u32[]{:S(2)}) copy-start(f32[512,1024]{1,0:T(8,128)} %get-tuple-element.253) | copy-start | bytes 6291460
  159.2 7.8 %copy-start.2 = (f32[3,512,1024]{2,1,0:T(8,128)S(1)}, f32[3,512,1024]{2,1,0:T(8,128)}, u32[]{:S(2)}) copy-start(f32[3,512,1024]{2,1,0:T(8,128)} %copy-done.1) | copy-start | bytes 18874372
  170.2 3.7 copy-start.11
  170.2 3.7 copy-start.14
  176.5 200.7 %reduce-scatter.6.cloned.1.call-start = ((), (), s32[]{:S(2)}) async-start(), calls=%async_computation.4 | async-start | bytes 122880 | tf_op jit(solution)/shard_map/reduce_scatter | solution.py:191
  278.7 66.6 %copy-start.9 = (f32[512,1024]{1,0:T(8,128)S(1)}, f32[512,1024]{1,0:T(8,128)}, u32[]{:S(2)}) copy-start(f32[512,1024]{1,0:T(8,128)} %get-tuple-element.258) | copy-start | bytes 6291460
  307.5 39.8 %copy-start.7 = (f32[512,1024]{1,0:T(8,128)S(1)}, f32[512,1024]{1,0:T(8,128)}, u32[]{:S(2)}) copy-start(f32[512,1024]{1,0:T(8,128)} %get-tuple-element.257) | copy-start | bytes 6291460
  345.3 4.1 copy-start.4
  347.3 4.1 copy-start.15
  349.4 3.9 copy-start.12
  357.7 240.4 %reduce-scatter.8.cloned.1.call-start = ((), (), s32[]{:S(2)}) async-start(), calls=%async_computation.5 | async-start | bytes 122880 | tf_op jit(solution)/shard_map/reduce_scatter | solution.py:191
  498.6 66.5 %copy-start.10 = (f32[512,1024]{1,0:T(8,128)S(1)}, f32[512,1024]{1,0:T(8,128)}, u32[]{:S(2)}) copy-start(f32[512,1024]{1,0:T(8,128)} %get-tuple-element.258) | copy-start | bytes 6291460
  527.4 39.7 %copy-start.8 = (f32[512,1024]{1,0:T(8,128)S(1)}, f32[512,1024]{1,0:T(8,128)}, u32[]{:S(2)}) copy-start(f32[512,1024]{1,0:T(8,128)} %get-tuple-element.257) | copy-start | bytes 6291460
  565.1 4.1 copy-start.5
  567.2 4.1 copy-start.16
  569.2 3.9 copy-start.13
Sparse Core Ops, SparseCore 0:
  176.6 18.7 reduce-scatter.3
  357.8 19.3 reduce-scatter.5
  577.6 20.4 reduce-scatter.7
